TPU v7x, 32 devices: a whole 2x2x4 slice. The times are simulated.
32 devices in a mesh: layer: 4 (over y, x), row: 2 (over core), col: 4 (over z).
Axes of the slice: x: 2, y: 2, z: 4, core: 2. Of those that a mesh axis runs over, the one named last changes fastest.
Arguments:
- hidden: bfloat16 [384, 2304], P(('layer', 'row')), may hold values from -60 to 60
- embedding: bfloat16 [16384, 2304], P(('row', 'col'), 'layer'), may hold values from -0.3 to 0.3
- teacher: bfloat16 [384, 16384], P('layer', ('row', 'col')), may hold values from -80 to 240
Outputs:
- grad_embedding: float32 [16384, 2304], P(('row', 'col'), 'layer')
- grad_hidden: float32 [384, 2304], P(('layer', 'row', 'col'))
All inputs are finite; a program needn't handle non-finite values.
Results may differ from a plain program's by a relative error of at most 0.0041.
Values may be sent and summed in bfloat16 or wider, within the bound.
A program may use at most 192 MiB of HBM per device.

v0:
```python
import jax
import jax.numpy as jnp
from jax import lax
from jax.sharding import PartitionSpec as P

LOSS_SCALE = 256


def local(hidden, embedding, teacher):
    token_rows = lax.all_gather(hidden, "row", axis=0, tiled=True)
    width_part = lax.all_to_all(token_rows, "layer", split_axis=1, concat_axis=0, tiled=True)
    logits = lax.psum_scatter(
        lax.dot_general(
            width_part, embedding, (((1,), (1,)), ((), ())), preferred_element_type=jnp.float32
        ),
        "layer",
        scatter_dimension=0,
        tiled=True,
    )
    teach_f = teacher.astype(jnp.float32)
    top_s, top_t = lax.pmax((jnp.max(logits, axis=1), jnp.max(teach_f, axis=1)), ("row", "col"))
    part_s = jnp.sum(jnp.exp(logits - top_s[:, None]), axis=1)
    part_t = jnp.sum(jnp.exp(teach_f - top_t[:, None]), axis=1)
    sum_s, sum_t = lax.psum((part_s, part_t), ("row", "col"))
    lse_s = top_s + jnp.log(sum_s)
    lse_t = top_t + jnp.log(sum_t)
    prob_s = jnp.exp(logits - lse_s[:, None])
    prob_t = jnp.exp(teach_f - lse_t[:, None])
    grads = ((prob_s - prob_t) * LOSS_SCALE).astype(jnp.bfloat16)
    grad_piece = lax.all_gather(grads, "layer", axis=0, tiled=True)
    embed_acc = lax.dot_general(
        grad_piece, width_part, (((0,), (0,)), ((), ())), preferred_element_type=jnp.float32
    )
    hidden_piece = jnp.dot(grad_piece, embedding, preferred_element_type=jnp.float32)
    hidden_terms = lax.all_to_all(hidden_piece, "layer", split_axis=0, concat_axis=1, tiled=True)
    grad_hidden = lax.psum_scatter(hidden_terms, ("row", "col"), scatter_dimension=0, tiled=True)
    return (embed_acc, grad_hidden)


def solution(mesh):
    placed = (P(("layer", "row"), None), P(("row", "col"), "layer"), P("layer", ("row", "col")))
    return jax.shard_map(
        local,
        mesh=mesh,
        in_specs=placed,
        out_specs=(P(("row", "col"), "layer"), P(("layer", "row", "col"), None)),
        check_vma=False,
    )
```

profile of v0, /device:TPU:0, one launch (start us, length us, event | category | flops | bytes accessed | tf_op | source)
XLA Modules:
  0.0 215.3 jit_solution(10763876937868347929)
XLA Ops:
  7.2 0.0 copy-start
  7.2 0.0 reduce-scatter.4.cloned.1.call-start
  7.2 2.6 %all_gather.6 = bf16[96,2304]{1,0:T(8,128)(2,1)S(1)} all-gather(bf16[48,2304]{1,0:T(8,128)(2,1)} %param.3), channel_id=1, replica_groups=mesh['layer'=4,'row'=2,'col'=4] {'row'}, dimensions={0}, use_global_device_ids=true | all-gather | bytes 663552 | tf_op jit(solution)/shard_map/all_gather | solution.py:10
  9.8 0.6 all_to_all.28
  10.4 0.1 copy.11
  10.5 13.4 %all_to_all.38 = bf16[96,4,576]{2,0,1:T(8,128)(2,1)S(1)} all-to-all(bf16[96,4,576]{2,0,1:T(8,128)(2,1)S(1)} %copy.11), channel_id=1, replica_groups=mesh['layer'=4,'row'=2,'col'=4] {'layer'}, dimensions={1} | all-to-all | bytes 884736 | tf_op jit(solution)/shard_map/all_to_all | solution.py:11
  23.9 0.0 copy-start.2
  23.9 0.8 copy-done.2
  24.7 0.0 copy-done
  24.7 3.1 %fusion.7 = f32[384,2048]{1,0:T(8,128)} fusion(bf16[384,576]{1,0:T(8,128)(2,1)S(1)} %bitcast.14, bf16[2048,576]{0,1:T(8,128)(2,1)S(1)} %copy-done), kind=kOutput, calls=%fused_computation.12 | convolution fusion | flops 905969664 | bytes 5947392 | tf_op jit(solution)/shard_map/dot_general | solution.py:13
  27.7 0.0 copy-start.5
  27.7 0.0 reduce-scatter.4.cloned.1.call-update
  27.8 0.0 all-gather.2.cloned.1.call-start
  27.8 0.9 copy-done.5
  28.7 0.2 reduce_max.24
  28.9 42.6 %reduce-scatter.4.cloned.1.call-done = f32[96,2048]{1,0:T(8,128)} async-done(((f32[384,2048]{1,0:T(8,128)}), f32[96,2048]{1,0:T(8,128)}) %reduce-scatter.4.cloned.1.call-update) | async-done | bytes 786448 | tf_op jit(solution)/shard_map/reduce_scatter | solution.py:12
  71.5 0.0 copy-start.1
  71.5 1.3 reduce_max.23
  72.8 16.6 %all-reduce.3 = (f32[96]{0:T(128)S(1)}, f32[96]{0:T(128)S(1)}) all-reduce(bf16[96]{0:T(256)(128)(2,1)S(1)} %reduce_max.24, f32[96]{0:T(128)S(1)} %reduce_max.23), channel_id=1, replica_groups=mesh['layer'=4,'row'=2,'col'=4] {'row','col'}, use_global_device_ids=true, to_apply=%region_6.0 | all-reduce | flops 192 | bytes 1344 | tf_op jit(solution)/shard_map/pmax | solution.py:21
  89.5 1.5 fusion.2
  91.0 14.2 %all-reduce.2 = (f32[96]{0:T(128)}, f32[96]{0:T(128)}) all-reduce(f32[96]{0:T(128)S(1)} %get-tuple-element.6, f32[96]{0:T(128)S(1)} %get-tuple-element.7), channel_id=1, replica_groups=mesh['layer'=4,'row'=2,'col'=4] {'row','col'}, use_global_device_ids=true, to_apply=%region_8.0 | all-reduce | flops 192 | bytes 1536 | tf_op jit(solution)/shard_map/psum | solution.py:24
  105.2 0.7 log_add_fusion
  105.9 0.7 log_add_fusion.1
  106.5 0.0 copy-done.1
  106.5 1.1 fusion.6
  107.6 0.0 all-gather.2.cloned.1.call-update
  107.6 0.0 copy-start.6
  107.6 31.0 %all-gather.2.cloned.1.call-done = bf16[384,2048]{1,0:T(8,128)(2,1)} async-done(((bf16[96,2048]{1,0:T(8,128)(2,1)}), bf16[384,2048]{1,0:T(8,128)(2,1)}) %all-gather.2.cloned.1.call-update) | async-done | bytes 1572880 | tf_op jit(solution)/shard_map/all_gather | solution.py:30
  138.6 3.8 %fusion.9 = f32[384,576]{1,0:T(8,128)} fusion(bf16[384,2048]{1,0:T(8,128)(2,1)} %all-gather.2.cloned.1.call-done, bf16[2048,576]{0,1:T(8,128)(2,1)S(1)} %copy-done), kind=kOutput, calls=%fused_computation.14 | convolution fusion | flops 905969664 | bytes 4816896 | tf_op jit(solution)/shard_map/dot_general | solution.py:34
  142.4 3.5 %all-to-all-start.1 = ((f32[4,96,576]{2,1,0:T(8,128)}), f32[4,96,576]{2,1,0:T(8,128)S(1)}, u32[]{:S(2)}, u32[]{:S(2)}) async-start(f32[4,96,576]{2,1,0:T(8,128)} %bitcast.17), calls=%async_computation.2 | async-start | bytes 1966080 | tf_op jit(solution)/shard_map/all_to_all | solution.py:35
  145.9 0.0 copy-done.6
  145.9 0.6 dynamic-slice.4
  147.2 11.8 %all-to-all-done.1 = f32[4,96,576]{2,1,0:T(8,128)S(1)} async-done(((f32[4,96,576]{2,1,0:T(8,128)}), f32[4,96,576]{2,1,0:T(8,128)S(1)}, u32[]{:S(2)}, u32[]{:S(2)}) %all-to-all-start.1) | async-done | bytes 884768 | tf_op jit(solution)/shard_map/all_to_all | solution.py:35
  158.9 0.0 copy-start.4
  158.9 0.9 copy-done.4
  159.9 0.0 copy-start.3
  159.9 2.8 %copy.13 = f32[96,4,576]{2,1,0:T(4,128)} copy(f32[96,4,576]{2,0,1:T(8,128)} %bitcast.16) | data formatting | bytes 1769472 | tf_op jit(solution)/shard_map/all_to_all | solution.py:35
  162.7 2.7 %all_to_all.35 = f32[96,2304]{1,0:T(8,128)} reshape(f32[96,4,576]{2,1,0:T(4,128)} %copy.13) | data formatting | bytes 1769472 | tf_op jit(solution)/shard_map/all_to_all | solution.py:35
  165.4 31.4 %fusion = f32[16,2304]{1,0:T(8,128)S(1)} fusion(f32[96,2304]{1,0:T(8,128)} %all_to_all.35), kind=kCustom, calls=%all-reduce-scatter | all-reduce-scatter fusion | flops 294913 | bytes 1032704
  196.8 2.1 collective-permute-start
  198.9 3.5 %collective-permute-start.1 = (f32[12,2304]{1,0:T(8,128)S(1)}, f32[12,2304]{1,0:T(8,128)S(1)}, u32[]{:S(2)}, u32[]{:S(2)}) collective-permute-start(f32[12,2304]{1,0:T(8,128)S(1)} %slice), channel_id=1, source_target_pairs={{0,2},{1,3},{2,4},{3,5},{4,6},{5,7},{8,10},{9,11},{10,12},{11,13},... | collective-permute-start | bytes 331784
  202.3 0.0 copy-done.3
  202.3 5.0 %fusion.8 = f32[2048,576]{0,1:T(8,128)} fusion(bf16[384,2048]{1,0:T(8,128)(2,1)} %all-gather.2.cloned.1.call-done, bf16[384,576]{1,0:T(8,128)(2,1)S(1)} %bitcast.15), kind=kOutput, calls=%fused_computation.13 | convolution fusion | flops 905969664 | bytes 6733824 | tf_op jit(solution)/shard_map/dot_general | solution.py:31
  207.4 0.0 collective-permute-done.1
  207.4 0.0 collective-permute-done
  207.4 0.4 concatenate
  207.8 0.7 constant_dynamic-slice_fusion
  (1 shorter events, 0.0 us)
Async XLA Ops:
  7.2 17.5 %copy-start = (bf16[2048,576]{0,1:T(8,128)(2,1)S(1)}, bf16[2048,576]{0,1:T(8,128)(2,1)}, u32[]{:S(2)}) copy-start(bf16[2048,576]{0,1:T(8,128)(2,1)} %param.4) | copy-start | bytes 7077892
  7.2 64.3 %reduce-scatter.4.cloned.1.call-start = ((), (), s32[]{:S(2)}) async-start(), calls=%async_computation.3 | async-start | bytes 3932160 | tf_op jit(solution)/shard_map/reduce_scatter | solution.py:12
  23.9 0.8 copy-start.2
  27.7 1.0 copy-start.5
  27.8 110.8 %all-gather.2.cloned.1.call-start = ((), (), s32[]{:S(2)}) async-start(), calls=%async_computation.4 | async-start | bytes 1966080 | tf_op jit(solution)/shard_map/all_gather | solution.py:30
  71.5 35.1 %copy-start.1 = (f32[96,2048]{1,0:T(8,128)S(1)}, f32[96,2048]{1,0:T(8,128)}, u32[]{:S(2)}) copy-start(f32[96,2048]{1,0:T(8,128)} %reduce-scatter.4.cloned.1.call-done) | copy-start | bytes 2359300
  107.6 38.3 %copy-start.6 = (u32[32]{0:T(128)S(1)}, u32[32]{0:T(128)}, u32[]{:S(2)}) copy-start(u32[32]{0:T(128)} %constant.10) | copy-start | bytes 388
  142.4 16.5 %all-to-all-start.1 = ((f32[4,96,576]{2,1,0:T(8,128)}), f32[4,96,576]{2,1,0:T(8,128)S(1)}, u32[]{:S(2)}, u32[]{:S(2)}) async-start(f32[4,96,576]{2,1,0:T(8,128)} %bitcast.17), calls=%async_computation.2 | async-start | bytes 1966080 | tf_op jit(solution)/shard_map/all_to_all | solution.py:35
  158.9 0.9 copy-start.4
  159.9 42.5 %copy-start.3 = (bf16[96,4,576]{2,0,1:T(8,128)(2,1)S(1)}, bf16[96,4,576]{2,0,1:T(8,128)(2,1)}, u32[]{:S(2)}) copy-start(bf16[96,4,576]{2,0,1:T(8,128)(2,1)} %copy-done.2) | copy-start | bytes 1327108
  196.8 10.6 %collective-permute-start = (f32[16,2304]{1,0:T(8,128)S(1)}, f32[16,2304]{1,0:T(8,128)S(1)}, u32[]{:S(2)}, u32[]{:S(2)}) collective-permute-start(f32[16,2304]{1,0:T(8,128)S(1)} %fusion), channel_id=1, source_target_pairs={{0,1},{1,2},{2,3},{3,4},{4,5},{5,6},{6,7},{8,9},{9,10},{10,11},{11... | collective-permute-start | bytes 442376
  198.9 8.5 %collective-permute-start.1 = (f32[12,2304]{1,0:T(8,128)S(1)}, f32[12,2304]{1,0:T(8,128)S(1)}, u32[]{:S(2)}, u32[]{:S(2)}) collective-permute-start(f32[12,2304]{1,0:T(8,128)S(1)} %slice), channel_id=1, source_target_pairs={{0,2},{1,3},{2,4},{3,5},{4,6},{5,7},{8,10},{9,11},{10,12},{11,13},... | collective-permute-start | bytes 331784
Sparse Core Ops, SparseCore 0:
  27.9 43.5 reduce-scatter.3
  107.7 30.8 all-gather.1
where the time goes:
time: 217 us; the launch traced here: 215 us
  waiting for transfers between devices  85.3 us (39%)
  blocking collectives  78.2 us (36%)
  between operations  14.8 us (7%)
  matrix products  11.9 us (5%)
  local copies, waits for them, and re-layouts  10.5 us (5%)
  starting transfers between devices  9.1 us (4%)
  other arithmetic  5.41 us (2%)
    reduce_scatter x1, waiting for transfers between devices, local(): lax.psum_scatter(lax.dot_general(width_part, embedding, (((1,), (1,)), ((...  42.6 us
    unnamed x1, blocking collectives  31.4 us
    all_gather x1, waiting for transfers between devices, local(): grad_piece = lax.all_gather(grads, 'layer', axis=0, tiled=True)  31 us
    pmax x1, blocking collectives, local(): lax.pmax((jnp.max(logits, axis=1), jnp.max(teach_f, axis=1)), ('row', 'co...  16.6 us
    psum x1, blocking collectives, local(): sum_s, sum_t = lax.psum((part_s, part_t), ('row', 'col'))  14.2 us
    all_to_all x1, blocking collectives, local(): lax.all_to_all(token_rows, 'layer', split_axis=1, concat_axis=0, tiled=True)  13.4 us
    all_to_all x1, waiting for transfers between devices, local(): lax.all_to_all(hidden_piece, 'layer', split_axis=0, concat_axis=1, tiled=...  11.8 us
    all_to_all x2, local copies, waits for them, and re-layouts, local(): lax.all_to_all(hidden_piece, 'layer', split_axis=0, concat_axis=1, tiled=...  5.53 us
  transfers between devices with their start and end apart: 5, of which 3 were waited for; matrix products, arithmetic and copies ran while one was open for 3% of the time, Pallas kernels for 0%

commit v1 on v0

v1 whole, which is shorter than its diff:
```python
import functools

import jax
import jax.numpy as jnp
from jax import lax
from jax.experimental import pallas as pl
from jax.experimental.pallas import tpu as pltpu
from jax.sharding import PartitionSpec as P

LOSS_SCALE = 256
LAYERS = 4
LANES = 128
MESH = pl.DeviceIdType.MESH
F32 = jnp.float32
BF16 = jnp.bfloat16


def kernel(nr, nc, h_ref, e_ref, t_ref, g_ref, wp_ref, gh_ref,
           hs, part, rx, ry, st_send, st_recv, hsend, hrecv, fsend,
           hid_s, hid_r, x_s, x_r, y_s, y_r, st_s, st_r, gx_s, gx_r, gy_s, gy_r,
           pc_s, pc_r, fin_s, fin_r):
    nl = LAYERS
    nrc = nr * nc
    rows, width = h_ref.shape[0], e_ref.shape[1]
    vocab = e_ref.shape[0]
    half = vocab // 2
    tok = t_ref.shape[0]
    q = tok // nrc
    l, r, c = lax.axis_index("layer"), lax.axis_index("row"), lax.axis_index("col")
    lx = l + 1 - 2 * (l % 2)
    ly = l + 2 - 4 * (l // 2)
    ld = 3 - l
    block = (l, lx, ly, ld)
    me = r * nc + c

    def remote(src, dst, ss, rs, dev):
        return pltpu.make_async_remote_copy(
            src_ref=src, dst_ref=dst, send_sem=ss, recv_sem=rs, device_id=dev, device_id_type=MESH)

    barrier = pltpu.get_barrier_semaphore()
    for d in range(nl):
        for jr in range(nr):
            if d or jr:
                pl.semaphore_signal(barrier, inc=1, device_id=(block[d], (r + jr) % nr, c), device_id_type=MESH)
    for jr in range(nr):
        for jc in range(1, nc):
            pl.semaphore_signal(barrier, inc=1, device_id=(l, (r + jr) % nr, (c + jc) % nc), device_id_type=MESH)

    for i in range(nl):
        hs[i] = h_ref[:, i * width:(i + 1) * width]
    wp_ref[l, r] = hs[l]
    pl.semaphore_wait(barrier, nl * nr - 1 + nr * (nc - 1))

    sends = []
    for d in (3, 1, 2, 0):
        for jr in range(nr):
            if d or jr:
                cp = remote(hs.at[block[d]], wp_ref.at[l, r], hid_s.at[d, jr], hid_r.at[d, jr],
                            (block[d], (r + jr) % nr, c))
                cp.start()
                sends.append(cp)

    def hidden_wait(d):
        for jr in range(nr):
            if d or jr:
                slot = wp_ref.at[block[d], (r + nr - jr) % nr]
                remote(slot, slot, hid_s.at[d, jr], hid_r.at[d, jr], (block[d], (r + jr) % nr, c)).wait_recv()

    def score(d, k):
        lhs = wp_ref[block[d]].reshape(nr * rows, width)
        part[d, k] = lax.dot_general(lhs, e_ref[k * half:(k + 1) * half, :], (((1,), (1,)), ((), ())),
                                     preferred_element_type=F32)

    def to_x(src, i):
        return remote(src, rx.at[i], x_s.at[i], x_r.at[i], (lx, r, c))

    def to_y(src, i):
        return remote(src, ry.at[i], y_s.at[i], y_r.at[i], (ly, r, c))

    hidden_wait(3)
    score(3, 0)
    x0 = to_x(part.at[3, 0], 0)
    x0.start()
    score(3, 1)
    y0 = to_y(part.at[3, 1], 0)
    y0.start()
    hidden_wait(1)
    score(1, 0)
    x1 = to_x(part.at[1, 0], 1)
    x1.start()
    hidden_wait(2)
    score(2, 1)
    y1 = to_y(part.at[2, 1], 1)
    y1.start()
    score(1, 1)
    score(2, 0)
    hidden_wait(0)
    score(0, 0)
    score(0, 1)

    teach = t_ref[...].astype(F32)
    top_t = jnp.max(teach, axis=1, keepdims=True)
    sum_t = jnp.sum(jnp.exp(teach - top_t), axis=1, keepdims=True)

    y0.wait_recv()
    part[1, 1] = part[1, 1] + ry[0]
    x2 = to_x(part.at[1, 1], 2)
    x2.start()
    x0.wait_recv()
    part[2, 0] = part[2, 0] + rx[0]
    y2 = to_y(part.at[2, 0], 2)
    y2.start()

    x1.wait_recv()
    part[0, 0] = part[0, 0] + rx[1]
    y1.wait_recv()
    part[0, 1] = part[0, 1] + ry[1]
    x2.wait_recv()
    part[0, 1] = part[0, 1] + rx[2]
    y2.wait_recv()
    part[0, 0] = part[0, 0] + ry[2]

    top_s = jnp.maximum(jnp.max(part[0, 0], axis=1, keepdims=True), jnp.max(part[0, 1], axis=1, keepdims=True))
    sum_s = (jnp.sum(jnp.exp(part[0, 0] - top_s), axis=1, keepdims=True)
             + jnp.sum(jnp.exp(part[0, 1] - top_s), axis=1, keepdims=True))
    tp = st_send.shape[1]
    lane = lax.broadcasted_iota(jnp.int32, (tok, LANES), 1)
    pack = jnp.where(lane == 0, top_s, jnp.where(lane == 1, sum_s, jnp.where(lane == 2, top_t, sum_t)))
    if tp > tok:
        pack = jnp.concatenate([pack, jnp.zeros((tp - tok, LANES), F32)], axis=0)
    st_send[...] = jnp.transpose(pack)[:8, :]
    st_recv[0] = st_send[...]

    def peer(j):
        k = (me + j) % nrc
        return (l, k // nc, k % nc)

    def stat_copy(j):
        return remote(st_send, st_recv.at[j], st_s.at[j], st_r.at[j], peer(j))

    @pl.loop(1, nrc)
    def _(j):
        stat_copy(j).start()

    @pl.loop(1, nrc)
    def _(j):
        stat_copy(j).wait_recv()

    tops = jnp.max(st_recv[...], axis=0)
    row_s = jnp.zeros((1, tp), F32)
    row_t = jnp.zeros((1, tp), F32)
    for j in range(nrc):
        row_s = row_s + st_recv[j, 1:2, :] * jnp.exp(st_recv[j, 0:1, :] - tops[0:1, :])
        row_t = row_t + st_recv[j, 3:4, :] * jnp.exp(st_recv[j, 2:3, :] - tops[2:3, :])
    lse_s = tops[0:1, :] + jnp.log(row_s)
    lse_t = tops[2:3, :] + jnp.log(row_t)
    sub = lax.broadcasted_iota(jnp.int32, (LANES, tp), 0)
    cols = jnp.transpose(jnp.where(sub == 0, lse_s, lse_t))
    lse_s = cols[:tok, 0:1]
    lse_t = cols[:tok, 1:2]

    def half_of(b, k):
        return g_ref.at[b, :, k * half:(k + 1) * half]

    def grad_x(b, k, i):
        return remote(half_of(b, k), half_of(b, k), gx_s.at[i], gx_r.at[i], (lx, r, c))

    def grad_y(b, k, i):
        return remote(half_of(b, k), half_of(b, k), gy_s.at[i], gy_r.at[i], (ly, r, c))

    for k in range(2):
        prob_s = jnp.exp(part[0, k] - lse_s)
        prob_t = jnp.exp(t_ref[:, k * half:(k + 1) * half].astype(F32) - lse_t)
        g_ref[l, :, k * half:(k + 1) * half] = ((prob_s - prob_t) * LOSS_SCALE).astype(BF16)
        if k == 0:
            sends.append(grad_x(l, 0, 0))
            sends[-1].start()
    for cp in (grad_y(l, 1, 0), grad_x(l, 1, 1), grad_y(l, 0, 1)):
        cp.start()
        sends.append(cp)

    def piece_copy(d, j):
        k = (me + j) % nrc
        return remote(hsend.at[d, k], hrecv.at[d, j], pc_s.at[d, j], pc_r.at[d, j], peer(j))

    def back(d):
        hp = jnp.dot(g_ref[block[d]], e_ref[...], preferred_element_type=F32)
        for k in range(nrc):
            hsend[d, k] = hp[k * q:(k + 1) * q, :]

        @pl.loop(1, nrc)
        def _(j):
            piece_copy(d, j).start()

    def finish(d):
        @pl.loop(1, nrc)
        def _(j):
            piece_copy(d, j).wait_recv()

        acc = hsend[d, me]
        for j in range(1, nrc):
            acc = acc + hrecv[d, j]
        if d == 0:
            gh_ref[l] = acc
        else:
            fsend[d] = acc
            cp = remote(fsend.at[d], gh_ref.at[l], fin_s.at[d], fin_r.at[d], (block[d], r, c))
            cp.start()
            sends.append(cp)

    back(0)
    grad_x(lx, 0, 0).wait_recv()
    cp = grad_y(lx, 0, 2)
    cp.start()
    sends.append(cp)
    grad_y(ly, 1, 0).wait_recv()
    cp = grad_x(ly, 1, 2)
    cp.start()
    sends.append(cp)
    finish(0)
    grad_x(lx, 1, 1).wait_recv()
    back(1)
    grad_y(ly, 0, 1).wait_recv()
    back(2)
    finish(1)
    finish(2)
    grad_x(ld, 1, 2).wait_recv()
    grad_y(ld, 0, 2).wait_recv()
    back(3)
    finish(3)
    for d in range(1, nl):
        remote(fsend.at[d], gh_ref.at[block[d]], fin_s.at[d], fin_r.at[d], (block[d], r, c)).wait_recv()

    for cp in sends + [x0, x1, x2, y0, y1, y2]:
        cp.wait_send()

    @pl.loop(1, nrc)
    def _(j):
        stat_copy(j).wait_send()
        for d in range(nl):
            piece_copy(d, j).wait_send()


def fused(nr, nc, hidden, embedding, teacher):
    nl = LAYERS
    nrc = nr * nc
    rows = hidden.shape[0]
    vocab, width = embedding.shape
    tok = teacher.shape[0]
    q = tok // nrc
    tp = -(-tok // LANES) * LANES
    dma = pltpu.SemaphoreType.DMA
    vmem = pl.BlockSpec(memory_space=pltpu.VMEM)
    return pl.pallas_call(
        functools.partial(kernel, nr, nc),
        out_shape=(
            jax.ShapeDtypeStruct((nl, tok, vocab), BF16),
            jax.ShapeDtypeStruct((nl, nr, rows, width), BF16),
            jax.ShapeDtypeStruct((nl, q, width), F32),
        ),
        in_specs=[vmem] * 3,
        out_specs=(vmem, vmem, vmem),
        scratch_shapes=[
            pltpu.VMEM((nl, rows, width), BF16),
            pltpu.VMEM((nl, 2, tok, vocab // 2), F32),
            pltpu.VMEM((3, tok, vocab // 2), F32),
            pltpu.VMEM((3, tok, vocab // 2), F32),
            pltpu.VMEM((8, tp), F32),
            pltpu.VMEM((nrc, 8, tp), F32),
            pltpu.VMEM((nl, nrc, q, width), F32),
            pltpu.VMEM((nl, nrc, q, width), F32),
            pltpu.VMEM((nl, q, width), F32),
            dma((nl, nr)), dma((nl, nr)),
            dma((3,)), dma((3,)), dma((3,)), dma((3,)),
            dma((nrc,)), dma((nrc,)),
            dma((3,)), dma((3,)), dma((3,)), dma((3,)),
            dma((nl, nrc)), dma((nl, nrc)),
            dma((nl,)), dma((nl,)),
        ],
        compiler_params=pltpu.CompilerParams(
            collective_id=0, has_side_effects=True, vmem_limit_bytes=62 * 1024 * 1024),
    )(hidden, embedding, teacher)


def solution(mesh):
    nl, nr, nc = mesh.shape["layer"], mesh.shape["row"], mesh.shape["col"]
    assert nl == LAYERS
    placed = (P(("layer", "row"), None), P(("row", "col"), "layer"), P("layer", ("row", "col")))

    def local(hidden, embedding, teacher):
        grads, width_part, pieces = fused(nr, nc, hidden, embedding, teacher)
        tokens = nl * teacher.shape[0]
        grad_embedding = lax.dot_general(
            grads.reshape(tokens, -1), width_part.reshape(tokens, -1),
            (((0,), (0,)), ((), ())), preferred_element_type=F32)
        grad_hidden = pieces.transpose(1, 0, 2).reshape(pieces.shape[1], -1)
        return grad_embedding, grad_hidden

    return jax.shard_map(
        local,
        mesh=mesh,
        in_specs=placed,
        out_specs=(P(("row", "col"), "layer"), P(("layer", "row", "col"), None)),
        check_vma=False,
    )
```

time: 217 us -> 97.1 us (0.45)
  waiting for transfers between devices: 85.3 us -> 0 us
  Pallas kernels: 0 us -> 85 us
  blocking collectives: 78.2 us -> 0 us
  between operations: 14.8 us -> 0.64 us
  starting transfers between devices: 9.1 us -> 0 us
  matrix products: 11.9 us -> 5.12 us
  other arithmetic: 5.41 us -> 0 us
  local copies, waits for them, and re-layouts: 10.5 us -> 6.09 us
    pallas_call x0 -> x1, Pallas kernels: none -> 85 us  [fused(): pl.pallas_call(functools.partial(kernel, nr, nc), out_shape=(jax.ShapeDty...]
    reduce_scatter x1 -> x0, waiting for transfers between devices: 42.6 us -> none  [local(): lax.psum_scatter(lax.dot_general(width_part, embedding, (((1,), (1,)), ((...]
    unnamed x1 -> x0, blocking collectives: 31.4 us -> none
    all_gather x1 -> x0, waiting for transfers between devices: 31 us -> none  [local(): grad_piece = lax.all_gather(grads, 'layer', axis=0, tiled=True)]
    pmax x1 -> x0, blocking collectives: 16.6 us -> none  [local(): lax.pmax((jnp.max(logits, axis=1), jnp.max(teach_f, axis=1)), ('row', 'co...]
    psum x1 -> x0, blocking collectives: 14.2 us -> none  [local(): sum_s, sum_t = lax.psum((part_s, part_t), ('row', 'col'))]
    all_to_all x1 -> x0, blocking collectives: 13.4 us -> none  [local(): lax.all_to_all(token_rows, 'layer', split_axis=1, concat_axis=0, tiled=True)]
    all_to_all x1 -> x0, waiting for transfers between devices: 11.8 us -> none  [local(): lax.all_to_all(hidden_piece, 'layer', split_axis=0, concat_axis=1, tiled=...]
  transfers between devices with their start and end apart: 5 -> 0, of which waited for: 3 -> 0; matrix products, arithmetic and copies ran while one was open for 3% -> 0% of each run, Pallas kernels for 0% -> 0%
where the time goes in v1:
time: 97.1 us; the launch traced here: 96.9 us
  Pallas kernels  85 us (88%)
  local copies, waits for them, and re-layouts  6.09 us (6%)
  matrix products  5.12 us (5%)
    pallas_call x1, Pallas kernels, fused(): pl.pallas_call(functools.partial(kernel, nr, nc), out_shape=(jax.ShapeDty...  85 us
    dot_general x1, matrix products, local(): lax.dot_general(grads.reshape(tokens, -1), width_part.reshape(tokens, -1)...  5.12 us
    unnamed x1, local copies, waits for them, and re-layouts  4.33 us

profile of v1, /device:TPU:0, one launch (start us, length us, event | category | flops | bytes accessed | tf_op | source)
XLA Modules:
  0.0 96.9 jit_solution(7529831403582584838)
XLA Ops:
  0.6 4.3 %copy.6.e_ref = bf16[2048,576]{1,0:T(8,128)(2,1)} copy(bf16[2048,576]{0,1:T(8,128)(2,1)} %param.4) | data formatting | bytes 4718592 | tf_op args[1]
  5.0 85.0 %shard_map.50 = (bf16[4,96,2048]{2,1,0:T(8,128)(2,1)}, bf16[4,2,48,576]{3,2,1,0:T(8,128)(2,1)}, f32[4,12,576]{2,1,0:T(8,128)}) custom-call(bf16[48,2304]{1,0:T(8,128)(2,1)} %h_ref.1, bf16[2048,576]{1,0:T(8,128)(2,1)} %copy.6.e_ref, bf16[96,2048]{1,0:T(8,128)(2,1)} %t_ref.1), custom_call_target="tpu_custom_call" | custom-call | tf_op jit(solution)/shard_map/pallas_call | solution.py:254
  90.0 1.0 copy.7
  91.0 0.8 reshape.15
  91.7 5.1 %fusion = f32[2048,576]{0,1:T(8,128)} fusion(bf16[384,2048]{1,0:T(8,128)(2,1)} %bitcast.5, bf16[384,576]{1,0:T(8,128)(2,1)} %bitcast.6), kind=kOutput, calls=%fused_computation | convolution fusion | flops 905969664 | bytes 6733824 | tf_op jit(solution)/shard_map/dot_general | solution.py:293

commit v2 on v1

--- a/solution.py
+++ b/solution.py
@@ -15,14 +15,15 @@
 BF16 = jnp.bfloat16
 
 
-def kernel(nr, nc, h_ref, e_ref, t_ref, g_ref, wp_ref, gh_ref,
-           hs, part, rx, ry, st_send, st_recv, hsend, hrecv, fsend,
-           hid_s, hid_r, x_s, x_r, y_s, y_r, st_s, st_r, gx_s, gx_r, gy_s, gy_r,
-           pc_s, pc_r, fin_s, fin_r):
+def kernel(nr, nc, h_in, e_in, t_in, g_out, wp_out, gh_ref,
+           h_ref, e_ref, t_ref, g_ref, wp_ref, ghs,
+           hs, part, rx, ry, st_send, st_recv, hsend, row_in, mid_sum, col_in, fsend,
+           in_sem, out_sem, hid_s, hid_r, x_s, x_r, y_s, y_r, st_s, st_r, gx_s, gx_r, gy_s, gy_r,
+           row_s, row_r, col_s, col_r, fin_s, fin_r):
     nl = LAYERS
     nrc = nr * nc
-    rows, width = h_ref.shape[0], e_ref.shape[1]
-    vocab = e_ref.shape[0]
+    rows = h_ref.shape[0]
+    width, vocab = e_ref.shape
     half = vocab // 2
     tok = t_ref.shape[0]
     q = tok // nrc
@@ -37,6 +38,17 @@
         return pltpu.make_async_remote_copy(
             src_ref=src, dst_ref=dst, send_sem=ss, recv_sem=rs, device_id=dev, device_id_type=MESH)
 
+    loads = [pltpu.make_async_copy(src, dst, in_sem.at[i])
+             for i, (src, dst) in enumerate(((h_in, h_ref), (e_in, e_ref), (t_in, t_ref)))]
+    for cp in loads:
+        cp.start()
+    stores = []
+
+    def store(src, dst):
+        cp = pltpu.make_async_copy(src, dst, out_sem.at[len(stores)])
+        cp.start()
+        stores.append(cp)
+
     barrier = pltpu.get_barrier_semaphore()
     for d in range(nl):
         for jr in range(nr):
@@ -46,30 +58,34 @@
         for jc in range(1, nc):
             pl.semaphore_signal(barrier, inc=1, device_id=(l, (r + jr) % nr, (c + jc) % nc), device_id_type=MESH)
 
+    loads[0].wait()
     for i in range(nl):
         hs[i] = h_ref[:, i * width:(i + 1) * width]
     wp_ref[l, r] = hs[l]
     pl.semaphore_wait(barrier, nl * nr - 1 + nr * (nc - 1))
 
     sends = []
-    for d in (3, 1, 2, 0):
-        for jr in range(nr):
-            if d or jr:
-                cp = remote(hs.at[block[d]], wp_ref.at[l, r], hid_s.at[d, jr], hid_r.at[d, jr],
-                            (block[d], (r + jr) % nr, c))
-                cp.start()
-                sends.append(cp)
+    for d in (3, 1, 2):
+        sends.append(remote(hs.at[block[d]], wp_ref.at[l, r], hid_s.at[d, 0], hid_r.at[d, 0], (block[d], r, c)))
+        sends[-1].start()
+
+    def hand_on(d):
+        slot = wp_ref.at[block[d], r]
+        if d:
+            remote(slot, slot, hid_s.at[d, 0], hid_r.at[d, 0], (block[d], r, c)).wait_recv()
+        for jr in range(1, nr):
+            src = slot if d else hs.at[l]
+            sends.append(remote(src, slot, hid_s.at[d, jr], hid_r.at[d, jr], (l, (r + jr) % nr, c)))
+            sends[-1].start()
 
     def hidden_wait(d):
-        for jr in range(nr):
-            if d or jr:
-                slot = wp_ref.at[block[d], (r + nr - jr) % nr]
-                remote(slot, slot, hid_s.at[d, jr], hid_r.at[d, jr], (block[d], (r + jr) % nr, c)).wait_recv()
+        for jr in range(1, nr):
+            slot = wp_ref.at[block[d], (r + nr - jr) % nr]
+            remote(slot, slot, hid_s.at[d, jr], hid_r.at[d, jr], (l, (r + jr) % nr, c)).wait_recv()
 
     def score(d, k):
         lhs = wp_ref[block[d]].reshape(nr * rows, width)
-        part[d, k] = lax.dot_general(lhs, e_ref[k * half:(k + 1) * half, :], (((1,), (1,)), ((), ())),
-                                     preferred_element_type=F32)
+        part[d, k] = jnp.dot(lhs, e_ref[:, k * half:(k + 1) * half], preferred_element_type=F32)
 
     def to_x(src, i):
         return remote(src, rx.at[i], x_s.at[i], x_r.at[i], (lx, r, c))
@@ -77,6 +93,9 @@
     def to_y(src, i):
         return remote(src, ry.at[i], y_s.at[i], y_r.at[i], (ly, r, c))
 
+    for d in (0, 3, 1, 2):
+        hand_on(d)
+    loads[1].wait()
     hidden_wait(3)
     score(3, 0)
     x0 = to_x(part.at[3, 0], 0)
@@ -98,6 +117,8 @@
     score(0, 0)
     score(0, 1)
 
+    store(wp_ref, wp_out)
+    loads[2].wait()
     teach = t_ref[...].astype(F32)
     top_t = jnp.max(teach, axis=1, keepdims=True)
     sum_t = jnp.sum(jnp.exp(teach - top_t), axis=1, keepdims=True)
@@ -147,13 +168,13 @@
         stat_copy(j).wait_recv()
 
     tops = jnp.max(st_recv[...], axis=0)
-    row_s = jnp.zeros((1, tp), F32)
-    row_t = jnp.zeros((1, tp), F32)
+    tot_s = jnp.zeros((1, tp), F32)
+    tot_t = jnp.zeros((1, tp), F32)
     for j in range(nrc):
-        row_s = row_s + st_recv[j, 1:2, :] * jnp.exp(st_recv[j, 0:1, :] - tops[0:1, :])
-        row_t = row_t + st_recv[j, 3:4, :] * jnp.exp(st_recv[j, 2:3, :] - tops[2:3, :])
-    lse_s = tops[0:1, :] + jnp.log(row_s)
-    lse_t = tops[2:3, :] + jnp.log(row_t)
+        tot_s = tot_s + st_recv[j, 1:2, :] * jnp.exp(st_recv[j, 0:1, :] - tops[0:1, :])
+        tot_t = tot_t + st_recv[j, 3:4, :] * jnp.exp(st_recv[j, 2:3, :] - tops[2:3, :])
+    lse_s = tops[0:1, :] + jnp.log(tot_s)
+    lse_t = tops[2:3, :] + jnp.log(tot_t)
     sub = lax.broadcasted_iota(jnp.int32, (LANES, tp), 0)
     cols = jnp.transpose(jnp.where(sub == 0, lse_s, lse_t))
     lse_s = cols[:tok, 0:1]
@@ -179,36 +200,50 @@
         cp.start()
         sends.append(cp)
 
-    def piece_copy(d, j):
-        k = (me + j) % nrc
-        return remote(hsend.at[d, k], hrecv.at[d, j], pc_s.at[d, j], pc_r.at[d, j], peer(j))
+    def row_copy(d, j):
+        to = (r + j) % nr
+        return remote(hsend.at[d, to], row_in.at[d, j], row_s.at[d, j], row_r.at[d, j], (l, to, c))
+
+    def col_copy(d, j):
+        to = (c + j) % nc
+        return remote(mid_sum.at[d, to], col_in.at[d, j], col_s.at[d, j], col_r.at[d, j], (l, r, to))
 
     def back(d):
-        hp = jnp.dot(g_ref[block[d]], e_ref[...], preferred_element_type=F32)
-        for k in range(nrc):
-            hsend[d, k] = hp[k * q:(k + 1) * q, :]
-
-        @pl.loop(1, nrc)
-        def _(j):
-            piece_copy(d, j).start()
+        store(g_ref.at[block[d]], g_out.at[block[d]])
+        hp = lax.dot_general(g_ref[block[d]], e_ref[...], (((1,), (1,)), ((), ())), preferred_element_type=F32)
+        for i in range(nr):
+            for k in range(nc):
+                at = (i * nc + k) * q
+                hsend[d, i, k] = hp[at:at + q, :]
+        for j in range(1, nr):
+            row_copy(d, j).start()
+
+    def middle(d):
+        for j in range(1, nr):
+            row_copy(d, j).wait_recv()
+        acc = hsend[d, r]
+        for j in range(1, nr):
+            acc = acc + row_in[d, j]
+        mid_sum[d] = acc
+        for j in range(1, nc):
+            col_copy(d, j).start()
 
     def finish(d):
-        @pl.loop(1, nrc)
-        def _(j):
-            piece_copy(d, j).wait_recv()
-
-        acc = hsend[d, me]
-        for j in range(1, nrc):
-            acc = acc + hrecv[d, j]
+        for j in range(1, nc):
+            col_copy(d, j).wait_recv()
+        acc = mid_sum[d, c]
+        for j in range(1, nc):
+            acc = acc + col_in[d, j]
         if d == 0:
-            gh_ref[l] = acc
+            ghs[l] = acc
         else:
             fsend[d] = acc
-            cp = remote(fsend.at[d], gh_ref.at[l], fin_s.at[d], fin_r.at[d], (block[d], r, c))
+            cp = remote(fsend.at[d], ghs.at[l], fin_s.at[d], fin_r.at[d], (block[d], r, c))
             cp.start()
             sends.append(cp)
 
     back(0)
+    middle(0)
     grad_x(lx, 0, 0).wait_recv()
     cp = grad_y(lx, 0, 2)
     cp.start()
@@ -222,14 +257,19 @@
     back(1)
     grad_y(ly, 0, 1).wait_recv()
     back(2)
+    middle(1)
+    middle(2)
     finish(1)
     finish(2)
     grad_x(ld, 1, 2).wait_recv()
     grad_y(ld, 0, 2).wait_recv()
     back(3)
+    middle(3)
     finish(3)
     for d in range(1, nl):
-        remote(fsend.at[d], gh_ref.at[block[d]], fin_s.at[d], fin_r.at[d], (block[d], r, c)).wait_recv()
+        remote(fsend.at[d], ghs.at[block[d]], fin_s.at[d], fin_r.at[d], (block[d], r, c)).wait_recv()
+    for i in range(nl):
+        gh_ref[:, i * width:(i + 1) * width] = ghs[i]
 
     for cp in sends + [x0, x1, x2, y0, y1, y2]:
         cp.wait_send()
@@ -237,44 +277,60 @@
     @pl.loop(1, nrc)
     def _(j):
         stat_copy(j).wait_send()
-        for d in range(nl):
-            piece_copy(d, j).wait_send()
+
+    for d in range(nl):
+        for j in range(1, nr):
+            row_copy(d, j).wait_send()
+        for j in range(1, nc):
+            col_copy(d, j).wait_send()
+    for cp in stores:
+        cp.wait()
 
 
 def fused(nr, nc, hidden, embedding, teacher):
     nl = LAYERS
     nrc = nr * nc
     rows = hidden.shape[0]
-    vocab, width = embedding.shape
+    width, vocab = embedding.shape
     tok = teacher.shape[0]
     q = tok // nrc
     tp = -(-tok // LANES) * LANES
     dma = pltpu.SemaphoreType.DMA
     vmem = pl.BlockSpec(memory_space=pltpu.VMEM)
+    hbm = pl.BlockSpec(memory_space=pl.ANY)
     return pl.pallas_call(
         functools.partial(kernel, nr, nc),
         out_shape=(
             jax.ShapeDtypeStruct((nl, tok, vocab), BF16),
             jax.ShapeDtypeStruct((nl, nr, rows, width), BF16),
-            jax.ShapeDtypeStruct((nl, q, width), F32),
+            jax.ShapeDtypeStruct((q, nl * width), F32),
         ),
-        in_specs=[vmem] * 3,
-        out_specs=(vmem, vmem, vmem),
+        in_specs=[hbm] * 3,
+        out_specs=(hbm, hbm, vmem),
         scratch_shapes=[
+            pltpu.VMEM((rows, nl * width), BF16),
+            pltpu.VMEM((width, vocab), BF16),
+            pltpu.VMEM((tok, vocab), BF16),
+            pltpu.VMEM((nl, tok, vocab), BF16),
+            pltpu.VMEM((nl, nr, rows, width), BF16),
+            pltpu.VMEM((nl, q, width), F32),
             pltpu.VMEM((nl, rows, width), BF16),
             pltpu.VMEM((nl, 2, tok, vocab // 2), F32),
             pltpu.VMEM((3, tok, vocab // 2), F32),
             pltpu.VMEM((3, tok, vocab // 2), F32),
             pltpu.VMEM((8, tp), F32),
             pltpu.VMEM((nrc, 8, tp), F32),
-            pltpu.VMEM((nl, nrc, q, width), F32),
-            pltpu.VMEM((nl, nrc, q, width), F32),
+            pltpu.VMEM((nl, nr, nc, q, width), F32),
+            pltpu.VMEM((nl, nr, nc, q, width), F32),
+            pltpu.VMEM((nl, nc, q, width), F32),
+            pltpu.VMEM((nl, nc, q, width), F32),
             pltpu.VMEM((nl, q, width), F32),
+            dma((3,)), dma((nl + 1,)),
             dma((nl, nr)), dma((nl, nr)),
             dma((3,)), dma((3,)), dma((3,)), dma((3,)),
             dma((nrc,)), dma((nrc,)),
             dma((3,)), dma((3,)), dma((3,)), dma((3,)),
-            dma((nl, nrc)), dma((nl, nrc)),
+            dma((nl, nr)), dma((nl, nr)), dma((nl, nc)), dma((nl, nc)),
             dma((nl,)), dma((nl,)),
         ],
         compiler_params=pltpu.CompilerParams(
@@ -288,12 +344,11 @@
     placed = (P(("layer", "row"), None), P(("row", "col"), "layer"), P("layer", ("row", "col")))
 
     def local(hidden, embedding, teacher):
-        grads, width_part, pieces = fused(nr, nc, hidden, embedding, teacher)
+        grads, width_part, grad_hidden = fused(nr, nc, hidden, embedding.T, teacher)
         tokens = nl * teacher.shape[0]
         grad_embedding = lax.dot_general(
             grads.reshape(tokens, -1), width_part.reshape(tokens, -1),
             (((0,), (0,)), ((), ())), preferred_element_type=F32)
-        grad_hidden = pieces.transpose(1, 0, 2).reshape(pieces.shape[1], -1)
         return grad_embedding, grad_hidden
 
     return jax.shard_map(

time: 97.1 us -> 83 us (0.85)
  Pallas kernels: 85 us -> 76.4 us
  local copies, waits for them, and re-layouts: 6.09 us -> 0.67 us
    pallas_call x1, Pallas kernels: 85 us -> 76.4 us  [fused(): pl.pallas_call(functools.partial(kernel, nr, nc), out_shape=(jax.ShapeDty...]
    unnamed x1 -> x3, local copies, waits for them, and re-layouts: 4.33 us -> 0.67 us
where the time goes in v2:
time: 83 us; the launch traced here: 82.8 us
  Pallas kernels  76.4 us (92%)
  matrix products  5.16 us (6%)
    pallas_call x1, Pallas kernels, fused(): pl.pallas_call(functools.partial(kernel, nr, nc), out_shape=(jax.ShapeDty...  76.4 us
    dot_general x1, matrix products, local(): lax.dot_general(grads.reshape(tokens, -1), width_part.reshape(tokens, -1)...  5.16 us

profile of v2, /device:TPU:0, one launch (start us, length us, event | category | flops | bytes accessed | tf_op | source)
XLA Modules:
  0.0 82.8 jit_solution(4187918213950217051)
XLA Ops:
  0.6 76.4 %shard_map.50 = (bf16[4,96,2048]{2,1,0:T(8,128)(2,1)}, bf16[4,2,48,576]{3,2,1,0:T(8,128)(2,1)}, f32[12,2304]{1,0:T(8,128)}) custom-call(bf16[48,2304]{1,0:T(8,128)(2,1)} %h_in.1, bf16[576,2048]{1,0:T(8,128)(2,1)} %bitcast.6, bf16[96,2048]{1,0:T(8,128)(2,1)} %t_in.1), custom_call_target="tpu_custom_call" | custom-call | tf_op jit(solution)/shard_map/pallas_call | solution.py:301
  77.0 0.0 copy-start
  77.0 5.2 %fusion = f32[2048,576]{0,1:T(8,128)} fusion(bf16[384,2048]{1,0:T(8,128)(2,1)} %bitcast.5, bf16[384,576]{1,0:T(8,128)(2,1)} %bitcast.7), kind=kOutput, calls=%fused_computation | convolution fusion | flops 905969664 | bytes 6733824 | tf_op jit(solution)/shard_map/dot_general | solution.py:349
  82.2 0.0 copy-done
  82.2 0.7 copy.6
Async XLA Ops:
  77.0 5.2 %copy-start = (f32[12,2304]{1,0:T(8,128)S(1)}, f32[12,2304]{1,0:T(8,128)}, u32[]{:S(2)}) copy-start(f32[12,2304]{1,0:T(8,128)} %get-tuple-element.11) | copy-start | bytes 331780

commit v3 on v2

--- a/solution.py
+++ b/solution.py
@@ -15,10 +15,10 @@
 BF16 = jnp.bfloat16
 
 
-def kernel(nr, nc, h_in, e_in, t_in, g_out, wp_out, gh_ref,
-           h_ref, e_ref, t_ref, g_ref, wp_ref, ghs,
+def kernel(nr, nc, h_in, e_in, t_in, ge_ref, gh_ref,
+           h_ref, e_ref, et_ref, t_ref, g_ref, wp_ref, wpt_ref, ghs,
            hs, part, rx, ry, st_send, st_recv, hsend, row_in, mid_sum, col_in, fsend,
-           in_sem, out_sem, hid_s, hid_r, x_s, x_r, y_s, y_r, st_s, st_r, gx_s, gx_r, gy_s, gy_r,
+           in_sem, hid_s, hid_r, x_s, x_r, y_s, y_r, st_s, st_r, gx_s, gx_r, gy_s, gy_r,
            row_s, row_r, col_s, col_r, fin_s, fin_r):
     nl = LAYERS
     nrc = nr * nc
@@ -42,13 +42,6 @@
              for i, (src, dst) in enumerate(((h_in, h_ref), (e_in, e_ref), (t_in, t_ref)))]
     for cp in loads:
         cp.start()
-    stores = []
-
-    def store(src, dst):
-        cp = pltpu.make_async_copy(src, dst, out_sem.at[len(stores)])
-        cp.start()
-        stores.append(cp)
-
     barrier = pltpu.get_barrier_semaphore()
     for d in range(nl):
         for jr in range(nr):
@@ -116,8 +109,11 @@
     hidden_wait(0)
     score(0, 0)
     score(0, 1)
-
-    store(wp_ref, wp_out)
+    piece = width // nl if (width // nl) % 16 == 0 else width
+    for i in range(0, width, piece):
+        et_ref[:, i:i + piece] = jnp.transpose(e_ref[i:i + piece, :])
+    wpt_ref[...] = jnp.transpose(wp_ref[...].reshape(nl * tok, width))
+
     loads[2].wait()
     teach = t_ref[...].astype(F32)
     top_t = jnp.max(teach, axis=1, keepdims=True)
@@ -209,8 +205,7 @@
         return remote(mid_sum.at[d, to], col_in.at[d, j], col_s.at[d, j], col_r.at[d, j], (l, r, to))
 
     def back(d):
-        store(g_ref.at[block[d]], g_out.at[block[d]])
-        hp = lax.dot_general(g_ref[block[d]], e_ref[...], (((1,), (1,)), ((), ())), preferred_element_type=F32)
+        hp = jnp.dot(g_ref[block[d]], et_ref[...], preferred_element_type=F32)
         for i in range(nr):
             for k in range(nc):
                 at = (i * nc + k) * q
@@ -241,6 +236,12 @@
             cp = remote(fsend.at[d], ghs.at[l], fin_s.at[d], fin_r.at[d], (block[d], r, c))
             cp.start()
             sends.append(cp)
+
+    def embed_part(lo, hi):
+        for i in range(lo, hi):
+            at = slice(i * vocab // 4, (i + 1) * vocab // 4)
+            ge_ref[:, at] = jnp.dot(wpt_ref[...], g_ref[:, :, at].reshape(nl * tok, vocab // 4),
+                                    preferred_element_type=F32)
 
     back(0)
     middle(0)
@@ -264,7 +265,9 @@
     grad_x(ld, 1, 2).wait_recv()
     grad_y(ld, 0, 2).wait_recv()
     back(3)
+    embed_part(0, 1)
     middle(3)
+    embed_part(1, 4)
     finish(3)
     for d in range(1, nl):
         remote(fsend.at[d], ghs.at[block[d]], fin_s.at[d], fin_r.at[d], (block[d], r, c)).wait_recv()
@@ -283,8 +286,6 @@
             row_copy(d, j).wait_send()
         for j in range(1, nc):
             col_copy(d, j).wait_send()
-    for cp in stores:
-        cp.wait()
 
 
 def fused(nr, nc, hidden, embedding, teacher):
@@ -301,18 +302,19 @@
     return pl.pallas_call(
         functools.partial(kernel, nr, nc),
         out_shape=(
-            jax.ShapeDtypeStruct((nl, tok, vocab), BF16),
-            jax.ShapeDtypeStruct((nl, nr, rows, width), BF16),
-            jax.ShapeDtypeStruct((q, nl * width), F32),
+            pltpu.VMEM((width, vocab), F32),
+            pltpu.VMEM((q, nl * width), F32),
         ),
         in_specs=[hbm] * 3,
-        out_specs=(hbm, hbm, vmem),
+        out_specs=(vmem, vmem),
         scratch_shapes=[
             pltpu.VMEM((rows, nl * width), BF16),
             pltpu.VMEM((width, vocab), BF16),
+            pltpu.VMEM((vocab, width), BF16),
             pltpu.VMEM((tok, vocab), BF16),
             pltpu.VMEM((nl, tok, vocab), BF16),
             pltpu.VMEM((nl, nr, rows, width), BF16),
+            pltpu.VMEM((width, nl * tok), BF16),
             pltpu.VMEM((nl, q, width), F32),
             pltpu.VMEM((nl, rows, width), BF16),
             pltpu.VMEM((nl, 2, tok, vocab // 2), F32),
@@ -325,7 +327,7 @@
             pltpu.VMEM((nl, nc, q, width), F32),
             pltpu.VMEM((nl, nc, q, width), F32),
             pltpu.VMEM((nl, q, width), F32),
-            dma((3,)), dma((nl + 1,)),
+            dma((3,)),
             dma((nl, nr)), dma((nl, nr)),
             dma((3,)), dma((3,)), dma((3,)), dma((3,)),
             dma((nrc,)), dma((nrc,)),
@@ -334,7 +336,7 @@
             dma((nl,)), dma((nl,)),
         ],
         compiler_params=pltpu.CompilerParams(
-            collective_id=0, has_side_effects=True, vmem_limit_bytes=62 * 1024 * 1024),
+            collective_id=0, has_side_effects=True, vmem_limit_bytes=56 * 1024 * 1024),
     )(hidden, embedding, teacher)
 
 
@@ -344,12 +346,8 @@
     placed = (P(("layer", "row"), None), P(("row", "col"), "layer"), P("layer", ("row", "col")))
 
     def local(hidden, embedding, teacher):
-        grads, width_part, grad_hidden = fused(nr, nc, hidden, embedding.T, teacher)
-        tokens = nl * teacher.shape[0]
-        grad_embedding = lax.dot_general(
-            grads.reshape(tokens, -1), width_part.reshape(tokens, -1),
-            (((0,), (0,)), ((), ())), preferred_element_type=F32)
-        return grad_embedding, grad_hidden
+        grad_embedding, grad_hidden = fused(nr, nc, hidden, embedding.T, teacher)
+        return grad_embedding.T, grad_hidden
 
     return jax.shard_map(
         local,

time: 83 us -> 78.6 us (0.947)
  matrix products: 5.16 us -> 0 us
  local copies, waits for them, and re-layouts: 0.67 us -> 2.85 us
  Pallas kernels: 76.4 us -> 75 us
    dot_general x1 -> x0, matrix products: 5.16 us -> none  [local(): lax.dot_general(grads.reshape(tokens, -1), width_part.reshape(tokens, -1)...]
    unnamed x3 -> x2, local copies, waits for them, and re-layouts: 0.67 us -> 2.85 us
    pallas_call x1, Pallas kernels: 76.4 us -> 75 us  [fused(): pl.pallas_call(functools.partial(kernel, nr, nc), out_shape=(pltpu.VMEM((...]
where the time goes in v3:
time: 78.6 us; the launch traced here: 78.4 us
  Pallas kernels  75 us (95%)
  local copies, waits for them, and re-layouts  2.85 us (4%)
    pallas_call x1, Pallas kernels, fused(): pl.pallas_call(functools.partial(kernel, nr, nc), out_shape=(pltpu.VMEM((...  75 us
    unnamed x2, local copies, waits for them, and re-layouts  2.85 us

profile of v3, /device:TPU:0, one launch (start us, length us, event | category | flops | bytes accessed | tf_op | source)
XLA Modules:
  0.0 78.4 jit_solution(13661596862830272761)
XLA Ops:
  0.6 75.0 %shard_map.50 = (f32[576,2048]{1,0:T(8,128)S(1)}, f32[12,2304]{1,0:T(8,128)S(1)}) custom-call(bf16[48,2304]{1,0:T(8,128)(2,1)} %h_in.1, bf16[576,2048]{1,0:T(8,128)(2,1)} %bitcast.3, bf16[96,2048]{1,0:T(8,128)(2,1)} %t_in.1), custom_call_target="tpu_custom_call" | custom-call | tf_op jit(solution)/shard_map/pallas_call | solution.py:302
  75.6 2.2 %copy.7 = f32[2048,576]{0,1:T(8,128)} copy(f32[2048,576]{0,1:T(8,128)S(1)} %bitcast.2) | data formatting | bytes 9437184
  77.8 0.7 copy.8

commit v4 on v3

--- a/solution.py
+++ b/solution.py
@@ -260,14 +260,15 @@
     back(2)
     middle(1)
     middle(2)
-    finish(1)
-    finish(2)
     grad_x(ld, 1, 2).wait_recv()
     grad_y(ld, 0, 2).wait_recv()
     back(3)
     embed_part(0, 1)
     middle(3)
-    embed_part(1, 4)
+    embed_part(1, 2)
+    finish(1)
+    finish(2)
+    embed_part(2, 4)
     finish(3)
     for d in range(1, nl):
         remote(fsend.at[d], ghs.at[block[d]], fin_s.at[d], fin_r.at[d], (block[d], r, c)).wait_recv()

time: 78.6 us -> 75.2 us (0.957)
  Pallas kernels: 75 us -> 71.5 us
    pallas_call x1, Pallas kernels: 75 us -> 71.5 us  [fused(): pl.pallas_call(functools.partial(kernel, nr, nc), out_shape=(pltpu.VMEM((...]
where the time goes in v4:
time: 75.2 us; the launch traced here: 75 us
  Pallas kernels  71.5 us (95%)
  local copies, waits for them, and re-layouts  2.85 us (4%)
    pallas_call x1, Pallas kernels, fused(): pl.pallas_call(functools.partial(kernel, nr, nc), out_shape=(pltpu.VMEM((...  71.5 us
    unnamed x2, local copies, waits for them, and re-layouts  2.85 us

profile of v4, /device:TPU:0, one launch (start us, length us, event | category | flops | bytes accessed | tf_op | source)
XLA Modules:
  0.0 75.0 jit_solution(8987737747934239050)
XLA Ops:
  0.6 71.5 %shard_map.50 = (f32[576,2048]{1,0:T(8,128)S(1)}, f32[12,2304]{1,0:T(8,128)S(1)}) custom-call(bf16[48,2304]{1,0:T(8,128)(2,1)} %h_in.1, bf16[576,2048]{1,0:T(8,128)(2,1)} %bitcast.3, bf16[96,2048]{1,0:T(8,128)(2,1)} %t_in.1), custom_call_target="tpu_custom_call" | custom-call | tf_op jit(solution)/shard_map/pallas_call | solution.py:303
  72.2 2.2 %copy.7 = f32[2048,576]{0,1:T(8,128)} copy(f32[2048,576]{0,1:T(8,128)S(1)} %bitcast.2) | data formatting | bytes 9437184
  74.4 0.7 copy.8
